TPU v7x, 32 devices: a whole 2x2x4 slice. The times are simulated.
32 devices in a mesh: sub: 4 (over x, core), gx: 8 (over z, y).
Axes of the slice: x: 2, y: 2, z: 4, core: 2. Of those that a mesh axis runs over, the one named last changes fastest.
Arguments:
- value_field: float32 [8, 64, 256, 256], P('sub', 'gx'), may hold values from -6 to 6
- speed_field: float32 [8, 64, 256, 256], P('sub', 'gx'), may hold values from 0.25 to 2
- drift_matrix: float32 [8, 3, 3], P('sub'), may hold values from -0.5 to 0.5
- drift_offset: float32 [8, 3], P('sub'), may hold values from -0.5 to 0.5
- control_bound: float32 [8, 3], P('sub'), may hold values from 0.5 to 1
- partner_table: int32 [8], replicated, may hold values from 0 to 7, as said below
- dropped_dim: int32 [8], P('sub'), may hold values from 1 to 2, as said below
Outputs:
- final_value: float32 [8, 64, 256, 256], P('sub', 'gx')
- shared_plane: float32 [8, 64, 256], P('sub', 'gx')
Inputs may be any that keep to these rules, and one draw needn't show every extreme that they name: `partner_table`: a permutation of the 8 subsystems that forms a single cycle through all of them, so no subsystem is its own partner. `dropped_dim`: half of the subsystems drop dimension 1 and half dimension 2.
All inputs are finite; a program needn't handle non-finite values.
Results may differ from a plain program's by a relative error of at most 0.00075.
Values sent between devices are 32-bit elements; how exact they have to be, the bound alone decides.
A program may use at most 128 MiB of HBM per device.

v0:
```python
import jax
import jax.numpy as jnp
from jax import lax
from jax.sharding import PartitionSpec as P

STEPS = 2


def padded_2(cells, sides, width):
    for axis, dim in sides:
        count = lax.axis_size(axis)
        head = lax.slice_in_dim(cells, 0, width, axis=dim)
        tail = lax.slice_in_dim(cells, cells.shape[dim] - width, cells.shape[dim], axis=dim)
        cells = jnp.concatenate(
            [
                lax.ppermute(tail, axis, [(i, (i + 1) % count) for i in range(count)]),
                cells,
                lax.ppermute(head, axis, [((i + 1) % count, i) for i in range(count)]),
            ],
            axis=dim,
        )
    return cells


def smaller(first, second):
    return jnp.where(jnp.abs(first) <= jnp.abs(second), first, second)


def one_sided(extended, dim_index, step_size):
    cell_count = extended.shape[dim_index] - 4

    def shifted(offset):
        return lax.slice_in_dim(extended, 2 + offset, 2 + offset + cell_count, axis=dim_index)

    back_two = shifted(-2)
    back_one = shifted(-1)
    middle = shifted(0)
    ahead_one = shifted(1)
    ahead_two = shifted(2)
    curve_back = back_two - 2.0 * back_one + middle
    curve_mid = back_one - 2.0 * middle + ahead_one
    curve_ahead = middle - 2.0 * ahead_one + ahead_two
    minus_side = (middle - back_one) / step_size + smaller(curve_back, curve_mid) / (
        2.0 * step_size
    )
    plus_side = (ahead_one - middle) / step_size - smaller(curve_mid, curve_ahead) / (
        2.0 * step_size
    )
    return (minus_side, plus_side)


def coordinates(first_row, cell_count, total_cells):
    indices = (first_row + jnp.arange(cell_count, dtype=jnp.int32)) % total_cells
    return -1.0 + (indices.astype(jnp.float32) + 0.5) * (2.0 / total_cells)


def advance(
    extended,
    speed_rows,
    first_coords,
    drift_matrix,
    drift_offset,
    control_bound,
    spacing,
    time_step,
):
    row_count = extended.shape[1] - 4
    grid_cells = extended.shape[2]
    center = lax.slice_in_dim(extended, 2, 2 + row_count, axis=1)
    gradients = [one_sided(extended, 1, spacing[0])]
    padded = jnp.pad(center, ((0, 0), (0, 0), (2, 2), (0, 0)), mode="edge")
    gradients.append(one_sided(padded, 2, spacing[1]))
    padded = jnp.pad(center, ((0, 0), (0, 0), (0, 0), (2, 2)), mode="edge")
    gradients.append(one_sided(padded, 3, spacing[2]))
    second_axis = coordinates(0, grid_cells, grid_cells)
    third_axis = coordinates(0, extended.shape[3], extended.shape[3])
    positions = (
        first_coords[None, :, None, None],
        second_axis[None, None, :, None],
        third_axis[None, None, None, :],
    )
    hamiltonian = jnp.zeros_like(center)
    for d in range(3):
        drift_term = drift_offset[:, d][:, None, None, None]
        for e in range(3):
            drift_term = drift_term + drift_matrix[:, d, e][:, None, None, None] * positions[e]
        minus_side, plus_side = gradients[d]
        average = 0.5 * (minus_side + plus_side)
        reach = control_bound[:, d][:, None, None, None] * speed_rows
        hamiltonian = (
            hamiltonian
            + drift_term * average
            - reach * jnp.abs(average)
            - (jnp.abs(drift_term) + reach) * 0.5 * (plus_side - minus_side)
        )
    return jnp.minimum(center, center - time_step * hamiltonian)


def on_device(
    value_field, speed_field, drift_matrix, drift_offset, control_bound, partner_table, dropped_dim
):
    local_subs = value_field.shape[0]
    local_rows = value_field.shape[1]
    grid_cells = value_field.shape[2]
    total_rows = local_rows * lax.axis_size("gx")
    spacing = (2.0 / total_rows, 2.0 / grid_cells, 2.0 / value_field.shape[3])
    time_step = min(spacing) / 15.0
    row_start = lax.axis_index("gx") * local_rows
    current = value_field
    first_coords = coordinates(row_start, local_rows, total_rows)
    for repeat in range(STEPS):
        extended = padded_2(current, (("gx", 1),), 2)
        current = advance(
            extended,
            speed_field,
            first_coords,
            drift_matrix,
            drift_offset,
            control_bound,
            spacing,
            time_step,
        )
    min_second = jnp.min(current, axis=2)
    min_third = jnp.min(current, axis=3)
    own_plane = jnp.where((dropped_dim == 1)[:, None, None], min_second, min_third)
    gathered = lax.all_gather(own_plane, "sub", axis=0, tiled=True)
    own_index = lax.axis_index("sub") * local_subs + jnp.arange(local_subs, dtype=jnp.int32)
    wanted = partner_table[own_index]
    selector = wanted[:, None] == jnp.arange(gathered.shape[0], dtype=jnp.int32)[None, :]
    partner_plane = jnp.sum(jnp.where(selector[:, :, None, None], gathered[None], 0.0), axis=1)
    return (current, jnp.maximum(own_plane, partner_plane))


def solution(mesh):
    return jax.shard_map(
        on_device,
        mesh=mesh,
        in_specs=(
            P("sub", "gx", None, None),
            P("sub", "gx", None, None),
            P("sub", None, None),
            P("sub", None),
            P("sub", None),
            P(),
            P("sub"),
        ),
        out_specs=(P("sub", "gx", None, None), P("sub", "gx", None)),
        check_vma=False,
    )
```

profile of v0, /device:TPU:0, one launch (start us, length us, event | category | flops | bytes accessed | tf_op | source)
XLA Modules:
  0.0 194.1 jit_solution(9191482264390488903)
XLA Ops:
  0.6 6.7 %constant_dynamic-update-slice_fusion.1 = (f32[2,10,256,256]{3,1,0,2:T(8,128)}, f32[2,8,256,256]{3,1,0,2:T(8,128)S(1)}) fusion(f32[2,8,256,256]{3,2,1,0:T(8,128)} %param.7), kind=kLoop, calls=%fused_computation.134 | loop fusion | bytes 12582912
  7.3 1.9 fusion.71
  9.3 6.0 %collective-permute-start.1 = (f32[2,2,256,256]{3,1,0,2:T(2,128)}, f32[2,2,256,256]{3,1,0,2:T(2,128)}, u32[]{:S(2)}, u32[]{:S(2)}) collective-permute-start(f32[2,2,256,256]{3,1,0,2:T(2,128)} %get-tuple-element.35), channel_id=1, source_target_pairs={{1,0},{2,1},{3,2},{4,3},{5,4},{6,5},{7,6},{0,7},{9,8},{10,9},{11,1... | collective-permute-start | bytes 3145736 | tf_op jit(solution)/shard_map/ppermute | solution.py:18
  15.3 2.1 %fusion.72 = (f32[2,8,256,1]{3,2,1,0:T(8,128)}, f32[2,8,256,1]{3,2,1,0:T(8,128)S(1)}) fusion(f32[2,8,256,256]{3,2,1,0:T(8,128)S(1)} %copy-done.4), kind=kLoop, calls=%fused_computation.180 | loop fusion | bytes 65536 | tf_op jit(solution)/shard_map/jit(_pad)/slice | solution.py:73
  18.2 0.8 copy.153
  19.2 2.2 %copy.173 = f32[2,8,256,1]{2,1,0,3:T(8,128)S(1)} copy(f32[2,8,256,1]{3,2,1,0:T(8,128)} %get-tuple-element.40) | data formatting | bytes 32768
  21.5 0.6 copy.174
  22.3 1.1 gather_fusion
  23.7 0.7 slice_bitcast_fusion.3
  24.8 1.5 broadcast_add_fusion
  26.3 31.9 %collective-permute-done.1 = f32[2,2,256,256]{3,1,0,2:T(2,128)} collective-permute-done((f32[2,2,256,256]{3,1,0,2:T(2,128)}, f32[2,2,256,256]{3,1,0,2:T(2,128)}, u32[]{:S(2)}, u32[]{:S(2)}) %collective-permute-start.1) | collective-permute-done | bytes 1048608 | tf_op jit(solution)/shard_map/ppermute | solution.py:18
  58.2 2.6 %constant_dynamic-update-slice_fusion = f32[2,10,256,256]{3,1,0,2:T(8,128)} fusion(f32[2,10,256,256]{3,1,0,2:T(8,128)} %get-tuple-element.36, f32[2,2,256,256]{3,1,0,2:T(2,128)} %collective-permute-done.1), kind=kLoop, calls=%fused_computation.133 | loop fusion | bytes 2097152 | tf_op jit(solution)/shard_map/concatenate | solution.py:14
  60.9 1.9 reshape.504
  62.8 2.0 %reshape.505 = f32[2,8,256,2]{3,1,0,2:T(8,128)} broadcast(f32[2,8,256]{1,0,2:T(2,128)S(1)} %copy.160), dimensions={0,1,2} | broadcast | bytes 49152 | tf_op jit(solution)/shard_map/jit(_pad)/reshape | solution.py:73
  64.8 30.2 %subtract_minimum_fusion.1 = f32[2,8,256,256]{3,1,0,2:T(8,128)S(1)} fusion(f32[2,8,256,256]{3,1,0,2:T(8,128)} %copy-done.3, f32[2,8,256,2]{3,1,0,2:T(8,128)} %reshape.505, f32[2,8,256,2]{3,1,0,2:T(8,128)} %reshape.504, f32[2,8,2,256]{3,1,0,2:T(8,128)S(1)} %reshape.503, f32[2,8,2,256]{3,1,0,2:T(8,128)S(1)} %reshape.502, ...), kind=kLoop, calls=%fused_computation.25 | loop fusion | flops 133169152 | bytes 22206488 | tf_op jit(solution)/shard_map/min | solution.py:96
  95.0 2.4 %fusion.69 = (f32[2,2,256,256]{3,1,0,2:T(2,128)}, f32[2,2,256,256]{3,1,0,2:T(2,128)}) fusion(f32[2,8,256,256]{3,1,0,2:T(8,128)S(1)} %subtract_minimum_fusion.1), kind=kLoop, calls=%fused_computation.177 | loop fusion | bytes 4194304 | tf_op jit(solution)/shard_map/slice | solution.py:13
  97.4 4.7 %collective-permute-start.3 = (f32[2,2,256,256]{3,1,0,2:T(2,128)}, f32[2,2,256,256]{3,1,0,2:T(2,128)}, u32[]{:S(2)}, u32[]{:S(2)}) collective-permute-start(f32[2,2,256,256]{3,1,0,2:T(2,128)} %get-tuple-element.29), channel_id=1, source_target_pairs={{1,0},{2,1},{3,2},{4,3},{5,4},{6,5},{7,6},{0,7},{9,8},{10,9},{11,1... | collective-permute-start | bytes 3145736 | tf_op jit(solution)/shard_map/ppermute | solution.py:18
  102.2 2.6 %fusion.70 = (f32[2,8,256,1]{3,1,0,2:T(8,128)}, f32[2,8,256,1]{3,1,0,2:T(8,128)}) fusion(f32[2,8,256,256]{3,1,0,2:T(8,128)S(1)} %subtract_minimum_fusion.1), kind=kLoop, calls=%fused_computation.178 | loop fusion | bytes 65536 | tf_op jit(solution)/shard_map/jit(_pad)/slice | solution.py:73
  104.8 2.5 %copy.167 = f32[2,8,256,1]{2,1,0,3:T(8,128)S(1)} copy(f32[2,8,256,1]{3,1,0,2:T(8,128)} %get-tuple-element.32) | data formatting | bytes 32768 | tf_op jit(solution)/shard_map/jit(_pad)/slice | solution.py:73
  107.3 0.9 copy.168
  108.2 2.5 %copy.169 = f32[2,8,256,1]{2,1,0,3:T(8,128)S(1)} copy(f32[2,8,256,1]{3,1,0,2:T(8,128)} %get-tuple-element.33) | data formatting | bytes 32768 | tf_op jit(solution)/shard_map/jit(_pad)/slice | solution.py:73
  110.7 0.8 copy.170
  111.5 0.9 slice_bitcast_fusion.1
  112.4 30.3 %collective-permute-done.2 = f32[2,2,256,256]{3,1,0,2:T(2,128)} collective-permute-done((f32[2,2,256,256]{3,1,0,2:T(2,128)}, f32[2,2,256,256]{3,1,0,2:T(2,128)}, u32[]{:S(2)}, u32[]{:S(2)}) %collective-permute-start.2) | collective-permute-done | bytes 1048608 | tf_op jit(solution)/shard_map/ppermute | solution.py:16
  142.8 2.7 %collective-permute-done.3 = f32[2,2,256,256]{3,1,0,2:T(2,128)} collective-permute-done((f32[2,2,256,256]{3,1,0,2:T(2,128)}, f32[2,2,256,256]{3,1,0,2:T(2,128)}, u32[]{:S(2)}, u32[]{:S(2)}) %collective-permute-start.3) | collective-permute-done | bytes 1048608 | tf_op jit(solution)/shard_map/ppermute | solution.py:18
  145.4 2.9 %reshape.508 = f32[2,8,256,2]{3,1,0,2:T(8,128)} broadcast(f32[2,8,256]{1,0,2:T(2,128)} %copy.168), dimensions={0,1,2} | broadcast | bytes 49152 | tf_op jit(solution)/shard_map/jit(_pad)/reshape | solution.py:73
  148.3 2.9 %reshape.509 = f32[2,8,256,2]{3,1,0,2:T(8,128)} broadcast(f32[2,8,256]{1,0,2:T(2,128)} %copy.170), dimensions={0,1,2} | broadcast | bytes 49152 | tf_op jit(solution)/shard_map/jit(_pad)/reshape | solution.py:73
  151.2 29.2 %fusion.68 = (f32[2,8,256]{1,0,2:T(2,128)}, f32[2,8,256]{2,1,0:T(8,128)S(1)}, f32[2,8,256,256]{3,1,0,2:T(8,128)}) fusion(f32[2,8,256,256]{3,1,0,2:T(8,128)S(1)} %copy-done.2, f32[2]{0:T(128)S(1)} %get-tuple-element.25, f32[2,8,256,2]{3,1,0,2:T(8,128)} %reshape.509, f32[2,8,256,2]{3,1,0,2:T(8,128)} %reshape.508, f32[2,256]{1,0:T(2,128)S(1)} %get-tuple-element.47, ...), kind=kLoop, calls=%fused_computation.176 | loop fusion | flops 137355264 | bytes 14899224 | tf_op jit(solution)/shard_map/reduce_min | solution.py:124
  180.4 1.0 copy.171
  181.5 5.2 %all_gather.3 = f32[8,8,256]{2,1,0:T(8,128)S(1)} all-gather(f32[2,8,256]{2,1,0:T(8,128)S(1)} %broadcast_select_fusion), channel_id=1, replica_groups=mesh['sub'=4,'gx'=8] {'sub'}, dimensions={0}, use_global_device_ids=true | all-gather | bytes 81920 | tf_op jit(solution)/shard_map/all_gather | solution.py:126
  186.9 0.6 max.3
  187.5 6.6 %copy.172 = f32[2,8,256,256]{3,2,1,0:T(8,128)} copy(f32[2,8,256,256]{3,1,0,2:T(8,128)} %get-tuple-element.27) | data formatting | bytes 8388608
  (45 shorter events, 2.1 us)
Async XLA Ops:
  0.6 21.7 %copy-start = (s32[8]{0:T(128)S(1)}, s32[8]{0:T(128)}, u32[]{:S(2)}) copy-start(s32[8]{0:T(128)} %param.12) | copy-start | bytes 100
  7.3 10.1 %copy-start.3 = (f32[2,8,256,256]{3,1,0,2:T(8,128)}, f32[2,8,256,256]{3,1,0,2:T(8,128)S(1)}, u32[]{:S(2)}) copy-start(f32[2,8,256,256]{3,1,0,2:T(8,128)S(1)} %get-tuple-element.37) | copy-start | bytes 12582916
  7.3 8.0 %copy-start.4 = (f32[2,8,256,256]{3,2,1,0:T(8,128)S(1)}, f32[2,8,256,256]{3,2,1,0:T(8,128)}, u32[]{:S(2)}) copy-start(f32[2,8,256,256]{3,2,1,0:T(8,128)} %param.7) | copy-start | bytes 12582916
  9.3 48.9 %collective-permute-start.1 = (f32[2,2,256,256]{3,1,0,2:T(2,128)}, f32[2,2,256,256]{3,1,0,2:T(2,128)}, u32[]{:S(2)}, u32[]{:S(2)}) collective-permute-start(f32[2,2,256,256]{3,1,0,2:T(2,128)} %get-tuple-element.35), channel_id=1, source_target_pairs={{1,0},{2,1},{3,2},{4,3},{5,4},{6,5},{7,6},{0,7},{9,8},{10,9},{11,1... | collective-permute-start | bytes 3145736 | tf_op jit(solution)/shard_map/ppermute | solution.py:18
  15.3 45.5 %collective-permute-start = (f32[2,2,256,256]{3,1,0,2:T(2,128)}, f32[2,2,256,256]{3,1,0,2:T(2,128)}, u32[]{:S(2)}, u32[]{:S(2)}) collective-permute-start(f32[2,2,256,256]{3,1,0,2:T(2,128)} %get-tuple-element.34), channel_id=1, source_target_pairs={{0,1},{1,2},{2,3},{3,4},{4,5},{5,6},{6,7},{7,0},{8,9},{9,10},{10,1... | collective-permute-start | bytes 3145736 | tf_op jit(solution)/shard_map/ppermute | solution.py:16
  15.3 2.2 %copy-start.5 = (f32[2,3,3]{2,0,1:T(2,128)S(1)}, f32[2,3,3]{2,0,1:T(2,128)}, u32[]{:S(2)}) copy-start(f32[2,3,3]{2,0,1:T(2,128)} %param.9) | copy-start | bytes 220
  15.3 2.4 %copy-start.6 = (f32[2,3]{1,0:T(2,128)S(1)}, f32[2,3]{1,0:T(2,128)}, u32[]{:S(2)}) copy-start(f32[2,3]{1,0:T(2,128)} %param.10) | copy-start | bytes 76
  17.5 6.0 %copy-start.7 = (f32[2,3]{1,0:T(2,128)S(1)}, f32[2,3]{1,0:T(2,128)}, u32[]{:S(2)}) copy-start(f32[2,3]{1,0:T(2,128)} %param.11) | copy-start | bytes 76
  94.9 9.9 %copy-start.1 = (f32[2,8,256,256]{3,1,0,2:T(8,128)}, f32[2,8,256,256]{3,1,0,2:T(8,128)S(1)}, u32[]{:S(2)}) copy-start(f32[2,8,256,256]{3,1,0,2:T(8,128)S(1)} %subtract_minimum_fusion.1) | copy-start | bytes 12582916
  94.9 7.2 %copy-start.9 = (s32[2]{0:T(128)S(1)}, s32[2]{0:T(128)}, u32[]{:S(2)}) copy-start(s32[2]{0:T(128)} %param.13) | copy-start | bytes 28
  95.0 7.2 %copy-start.8 = (s32[2]{0:T(128)S(1)}, s32[2]{0:T(128)}, u32[]{:S(2)}) copy-start(s32[2]{0:T(128)} %gather_fusion) | copy-start | bytes 28
  97.4 45.4 %collective-permute-start.2 = (f32[2,2,256,256]{3,1,0,2:T(2,128)}, f32[2,2,256,256]{3,1,0,2:T(2,128)}, u32[]{:S(2)}, u32[]{:S(2)}) collective-permute-start(f32[2,2,256,256]{3,1,0,2:T(2,128)} %get-tuple-element.28), channel_id=1, source_target_pairs={{0,1},{1,2},{2,3},{3,4},{4,5},{5,6},{6,7},{7,0},{8,9},{9,10},{10,1... | collective-permute-start | bytes 3145736 | tf_op jit(solution)/shard_map/ppermute | solution.py:16
  97.4 48.1 %collective-permute-start.3 = (f32[2,2,256,256]{3,1,0,2:T(2,128)}, f32[2,2,256,256]{3,1,0,2:T(2,128)}, u32[]{:S(2)}, u32[]{:S(2)}) collective-permute-start(f32[2,2,256,256]{3,1,0,2:T(2,128)} %get-tuple-element.29), channel_id=1, source_target_pairs={{1,0},{2,1},{3,2},{4,3},{5,4},{6,5},{7,6},{0,7},{9,8},{10,9},{11,1... | collective-permute-start | bytes 3145736 | tf_op jit(solution)/shard_map/ppermute | solution.py:18
  111.5 39.7 %copy-start.2 = (f32[2,8,256,256]{3,1,0,2:T(8,128)S(1)}, f32[2,8,256,256]{3,1,0,2:T(8,128)}, u32[]{:S(2)}) copy-start(f32[2,8,256,256]{3,1,0,2:T(8,128)} %copy-done.1) | copy-start | bytes 12582916
where the time goes:
time: 195 us; the launch traced here: 194 us
  waiting for transfers between devices  64.9 us (33%)
  other arithmetic  62.2 us (32%)
  local copies, waits for them, and re-layouts  50.2 us (26%)
  starting transfers between devices  10.8 us (6%)
  blocking collectives  5.23 us (3%)
    ppermute x2, waiting for transfers between devices, padded_2(): lax.ppermute(head, axis, [((i + 1) % count, i) for i in range(count)])  34.6 us
    ppermute x2, waiting for transfers between devices, padded_2(): lax.ppermute(tail, axis, [(i, (i + 1) % count) for i in range(count)])  30.3 us
    min x1, other arithmetic, advance(): return jnp.minimum(center, center - time_step * hamiltonian)  30.2 us
    reduce_min x1, other arithmetic, on_device(): min_third = jnp.min(current, axis=3)  29.2 us
    unnamed x24, local copies, waits for them, and re-layouts  16.2 us
    slice x8, local copies, waits for them, and re-layouts, advance(): padded = jnp.pad(center, ((0, 0), (0, 0), (0, 0), (2, 2)), mode='edge')  11.8 us
    ppermute x2, starting transfers between devices, padded_2(): lax.ppermute(head, axis, [((i + 1) % count, i) for i in range(count)])  10.8 us
    reshape x4, local copies, waits for them, and re-layouts, advance(): padded = jnp.pad(center, ((0, 0), (0, 0), (0, 0), (2, 2)), mode='edge')  9.68 us
  transfers between devices with their start and end apart: 4, of which 3 were waited for; matrix products, arithmetic and copies ran while one was open for 12% of the time, Pallas kernels for 0%

commit v1 on v0

v1 whole, which is shorter than its diff:
```python
import functools

import jax
import jax.numpy as jnp
from jax import lax
from jax.experimental import pallas as pl
from jax.experimental.pallas import tpu as pltpu
from jax.sharding import PartitionSpec as P

STEPS = 2
PAD = 8
LANES = 128
MESH = pl.DeviceIdType.MESH


def pick(first, second, first_size, second_size):
    return 0.5 * jnp.where(first_size <= second_size, first, second)


def sides(cells):
    slopes = [b - a for a, b in zip(cells[:-1], cells[1:])]
    curves = [b - a for a, b in zip(slopes[:-1], slopes[1:])]
    sizes = [jnp.abs(c) for c in curves]
    picks = [
        pick(curves[k], curves[k + 1], sizes[k], sizes[k + 1]) for k in range(len(curves) - 1)
    ]
    return [
        (slopes[k + 1] + picks[k], picks[k + 1] - slopes[k + 2]) for k in range(len(picks) - 1)
    ]


def lane_shift(parts, step, ends):
    lane = lax.broadcasted_iota(jnp.int32, parts[0].shape, 1)
    rolled = [pltpu.roll(p, (LANES - step) % LANES, 1) for p in parts]
    count = len(parts)
    if step == 1:
        at_end = lane == LANES - 1
        after = [rolled[i + 1] if i + 1 < count else ends for i in range(count)]
    else:
        at_end = lane == 0
        after = [rolled[i - 1] if i > 0 else ends for i in range(count)]
    return [jnp.where(at_end, after[i], rolled[i]) for i in range(count)]


def lane_sides(parts):
    zero = jnp.zeros_like(parts[0])
    ahead = lane_shift(parts, 1, parts[-1])
    slopes = [a - v for a, v in zip(ahead, parts)]
    back_slopes = lane_shift(slopes, -1, zero)
    curves = [a - b for a, b in zip(slopes, back_slopes)]
    back_curves = lane_shift(curves, -1, zero)
    picks = [pick(b, c, jnp.abs(b), jnp.abs(c)) for b, c in zip(back_curves, curves)]
    ahead_picks = lane_shift(picks, 1, zero)
    return [(b + q, a - s) for b, q, a, s in zip(back_slopes, picks, ahead_picks, slopes)]


def kernel(
    gx_name,
    sub_name,
    value,
    speed_in,
    matrix,
    offset,
    bound,
    partner,
    dropped,
    final,
    shared,
    first,
    second,
    speed,
    result,
    minima,
    own,
    gathered,
    load_sem,
    speed_sem,
    out_sem,
    send_sem,
    recv_sem,
    plane_send,
    plane_recv,
):
    subs, rows, cells_y, cells_z = value.shape
    halves = cells_z // LANES
    count = lax.axis_size(gx_name)
    me = lax.axis_index(gx_name)
    sub_count = lax.axis_size(sub_name)
    sub_me = lax.axis_index(sub_name)
    total_rows = rows * count
    spacing = (2.0 / total_rows, 2.0 / cells_y, 2.0 / cells_z)
    time_step = min(spacing) / 15.0
    scale = [time_step / h for h in spacing]
    targets = (lax.rem(me + 1, count), lax.rem(me + count - 1, count))
    body = pl.ds(PAD, cells_y)

    loads = {}
    for s in range(subs):
        for h in range(halves):
            copy = pltpu.make_async_copy(
                value.at[s, :, :, pl.ds(h * LANES, LANES)],
                first.at[s, pl.ds(2, rows), h, body, :],
                load_sem.at[s, h],
            )
            copy.start()
            loads[s, h] = copy
        copy = pltpu.make_async_copy(speed_in.at[s], speed.at[s], speed_sem.at[s])
        copy.start()
        loads[s] = copy

    barrier = pltpu.get_barrier_semaphore()
    for target in targets:
        pl.semaphore_signal(barrier, inc=1, device_id={gx_name: target}, device_id_type=MESH)
    for k in range(1, sub_count):
        peer = lax.rem(sub_me + k, sub_count)
        pl.semaphore_signal(barrier, inc=1, device_id={sub_name: peer}, device_id_type=MESH)
    pl.semaphore_wait(barrier, 2 + sub_count - 1)

    sends = {}

    def send(step, s, side):
        for h in range(halves):
            start = rows - 2 if side == 0 else 0
            land = 0 if side == 0 else rows + 2
            if step == 0:
                source = value.at[s, pl.ds(start, 2), :, pl.ds(h * LANES, LANES)]
                sink = first.at[s, pl.ds(land, 2), h, body, :]
            else:
                source = second.at[s, pl.ds(start + 2, 2), h, body, :]
                sink = second.at[s, pl.ds(land, 2), h, body, :]
            copy = pltpu.make_async_remote_copy(
                src_ref=source,
                dst_ref=sink,
                send_sem=send_sem.at[step, s, side, h],
                recv_sem=recv_sem.at[step, s, side, h],
                device_id={gx_name: targets[side]},
                device_id_type=MESH,
            )
            copy.start()
            sends[step, s, side, h] = copy

    def receive(step, s, side):
        for h in range(halves):
            sends[step, s, side, h].wait_recv()

    for s in range(subs):
        for side in (0, 1):
            send(0, s, side)

    def pad_rows(ref, s, start, planes):
        for p in range(start, start + planes):
            for h in range(halves):
                low = ref[s, p, h, pl.ds(PAD, 1), :]
                ref[s, p, h, pl.ds(0, PAD), :] = jnp.broadcast_to(low, (PAD, LANES))
                high = ref[s, p, h, pl.ds(PAD + cells_y - 1, 1), :]
                ref[s, p, h, pl.ds(PAD + cells_y, PAD), :] = jnp.broadcast_to(high, (PAD, LANES))

    tile = (8, LANES)
    lane_index = lax.broadcasted_iota(jnp.int32, tile, 1)
    row_index = lax.broadcasted_iota(jnp.int32, tile, 0)
    z_at = [
        -1.0 + ((lane_index + h * LANES).astype(jnp.float32) + 0.5) * (2.0 / cells_z)
        for h in range(halves)
    ]

    def compute(step, s, start, planes):
        source = first if step == 0 else second
        reach = [bound[s, d] * scale[d] for d in range(3)]
        z_part = [[z * (matrix[s, d, 2] * scale[d]) for z in z_at] for d in range(3)]
        base = []
        for p in range(start, start + planes):
            x = -1.0 + ((me * rows + p).astype(jnp.float32) + 0.5) * (2.0 / total_rows)
            base.append([(offset[s, d] + matrix[s, d, 0] * x) * scale[d] for d in range(3)])

        def block(r, lows):
            at = pl.multiple_of(r * 8, 8)
            y = -1.0 + ((row_index + at).astype(jnp.float32) + 0.5) * (2.0 / cells_y)
            yz_part = []
            for d in range(3):
                y_part = y * (matrix[s, d, 1] * scale[d])
                yz_part.append([z + y_part for z in z_part[d]])
            lines = [
                [
                    source[s, p, h, pl.ds(PAD + at, 8), :]
                    for p in range(start, start + planes + 4)
                ]
                for h in range(halves)
            ]
            along_x = [sides(line) for line in lines]
            new_lows = []
            for p in range(planes):
                parts = [lines[h][p + 2] for h in range(halves)]
                along_z = lane_sides(parts)
                new = []
                for h in range(halves):
                    around = [
                        parts[h]
                        if k == 0
                        else source[s, start + p + 2, h, pl.ds(PAD + at + k, 8), :]
                        for k in (-2, -1, 0, 1, 2)
                    ]
                    along_y = sides(around)[0]
                    drift_sum = None
                    reach_sum = None
                    for d, (minus, plus_neg) in enumerate((along_x[h][p], along_y, along_z[h])):
                        drift = yz_part[d][h] + base[p][d]
                        term = jnp.abs(drift) * jnp.where(drift >= 0.0, minus, plus_neg)
                        least = reach[d] * jnp.minimum(minus, plus_neg)
                        drift_sum = term if d == 0 else drift_sum + term
                        reach_sum = least if d == 0 else reach_sum + least
                    rate = speed[s, start + p, pl.ds(at, 8), pl.ds(h * LANES, LANES)]
                    hamiltonian = drift_sum + rate * reach_sum
                    new.append(parts[h] - jnp.maximum(hamiltonian, 0.0))
                for h in range(halves):
                    if step == 0:
                        second[s, start + p + 2, h, pl.ds(PAD + at, 8), :] = new[h]
                    else:
                        result[s, start + p, pl.ds(at, 8), pl.ds(h * LANES, LANES)] = new[h]
                        new_lows.append(jnp.minimum(lows[p * halves + h], new[h]))
                if step == 1:
                    minima[p, pl.ds(at, 8), :] = functools.reduce(jnp.minimum, new)
            return tuple(new_lows)

        if step == 0:
            lax.fori_loop(0, cells_y // 8, block, ())
            pad_rows(second, s, start + 2, planes)
            return
        lows = tuple(jnp.full(tile, jnp.inf, jnp.float32) for _ in range(planes * halves))
        lows = lax.fori_loop(0, cells_y // 8, block, lows)
        copy = pltpu.make_async_copy(
            result.at[s, pl.ds(start, planes)],
            final.at[s, pl.ds(start, planes)],
            out_sem.at[s, start // 2],
        )
        copy.start()
        outs.append(copy)
        drops_second = dropped[s] == 1
        for p in range(planes):
            by_second = jnp.concatenate(
                [
                    jnp.min(lows[p * halves + h], axis=0, keepdims=True) for h in range(halves)
                ],
                axis=1,
            )
            by_third = jnp.min(minima[p].T, axis=0, keepdims=True)
            own[s, pl.ds(start + p, 1), :] = jnp.where(drops_second, by_second, by_third)

    outs = []
    last = rows - 2
    for s in range(subs):
        for h in range(halves):
            loads[s, h].wait()
        pad_rows(first, s, 2, rows)
        loads[s].wait()
        for start in range(2, last, 2):
            compute(0, s, start, 2)

    for s in range(subs):
        receive(0, s, 0)
        compute(0, s, 0, 2)
        send(1, s, 1)
        receive(0, s, 1)
        compute(0, s, last, 2)
        send(1, s, 0)
    for s in range(subs):
        for start in range(2, last, 2):
            compute(1, s, start, 2)

    plane_sends = []
    for s in range(subs):
        receive(1, s, 1)
        compute(1, s, last, 2)
        receive(1, s, 0)
        compute(1, s, 0, 2)
        gathered[sub_me * subs + s] = own[s]
        for k in range(1, sub_count):
            copy = pltpu.make_async_remote_copy(
                src_ref=own.at[s],
                dst_ref=gathered.at[sub_me * subs + s],
                send_sem=plane_send.at[s, k - 1],
                recv_sem=plane_recv.at[s, k - 1],
                device_id={sub_name: lax.rem(sub_me + k, sub_count)},
                device_id_type=MESH,
            )
            copy.start()
            plane_sends.append(copy)
    for copy in sends.values():
        copy.wait_send()
    for copy in plane_sends:
        copy.wait()
    for s in range(subs):
        shared[s] = jnp.maximum(own[s], gathered[partner[sub_me * subs + s]])
    for copy in outs:
        copy.wait()


def on_device(
    value_field, speed_field, drift_matrix, drift_offset, control_bound, partner_table, dropped_dim
):
    subs, rows, cells_y, cells_z = value_field.shape
    halves = cells_z // LANES
    sub_count = lax.axis_size("sub")
    hbm = pl.BlockSpec(memory_space=pl.ANY)
    smem = pl.BlockSpec(memory_space=pltpu.SMEM)
    vmem = pl.BlockSpec(memory_space=pltpu.VMEM)
    field = (subs, rows + 4, halves, cells_y + 2 * PAD, LANES)
    return pl.pallas_call(
        functools.partial(kernel, "gx", "sub"),
        out_shape=(
            jax.ShapeDtypeStruct(value_field.shape, jnp.float32),
            jax.ShapeDtypeStruct((subs, rows, cells_z), jnp.float32),
        ),
        in_specs=[hbm, hbm, smem, smem, smem, smem, smem],
        out_specs=(hbm, vmem),
        scratch_shapes=[
            pltpu.VMEM(field, jnp.float32),
            pltpu.VMEM(field, jnp.float32),
            pltpu.VMEM(value_field.shape, jnp.float32),
            pltpu.VMEM(value_field.shape, jnp.float32),
            pltpu.VMEM((2, cells_y, LANES), jnp.float32),
            pltpu.VMEM((subs, rows, cells_z), jnp.float32),
            pltpu.VMEM((subs * sub_count, rows, cells_z), jnp.float32),
            pltpu.SemaphoreType.DMA((subs, halves)),
            pltpu.SemaphoreType.DMA((subs,)),
            pltpu.SemaphoreType.DMA((subs, rows // 2)),
            pltpu.SemaphoreType.DMA((STEPS, subs, 2, halves)),
            pltpu.SemaphoreType.DMA((STEPS, subs, 2, halves)),
            pltpu.SemaphoreType.DMA((subs, sub_count - 1)),
            pltpu.SemaphoreType.DMA((subs, sub_count - 1)),
        ],
        compiler_params=pltpu.CompilerParams(
            collective_id=0, has_side_effects=True, vmem_limit_bytes=56 * 1024 * 1024
        ),
    )(
        value_field,
        speed_field,
        drift_matrix,
        drift_offset,
        control_bound,
        partner_table,
        dropped_dim,
    )


def solution(mesh):
    return jax.shard_map(
        on_device,
        mesh=mesh,
        in_specs=(
            P("sub", "gx", None, None),
            P("sub", "gx", None, None),
            P("sub", None, None),
            P("sub", None),
            P("sub", None),
            P(),
            P("sub"),
        ),
        out_specs=(P("sub", "gx", None, None), P("sub", "gx", None)),
        check_vma=False,
    )
```

time: 195 us -> 170 us (0.87)
  Pallas kernels: 0 us -> 163 us
  waiting for transfers between devices: 64.9 us -> 0 us
  other arithmetic: 62.2 us -> 0 us
  local copies, waits for them, and re-layouts: 50.2 us -> 6.49 us
  starting transfers between devices: 10.8 us -> 0 us
  blocking collectives: 5.23 us -> 0 us
    pallas_call x0 -> x1, Pallas kernels: none -> 163 us  [on_device(): pl.pallas_call(functools.partial(kernel, 'gx', 'sub'), out_shape=(jax.Sha...]
    ppermute x4 -> x0, waiting for transfers between devices: 64.9 us -> none  [the longest x2 34.6 us: padded_2(): lax.ppermute(head, axis, [((i + 1) % count, i) for i in range(count)])]
    min x1 -> x0, other arithmetic: 30.2 us -> none  [advance(): return jnp.minimum(center, center - time_step * hamiltonian)]
    reduce_min x1 -> x0, other arithmetic: 29.2 us -> none  [on_device(): min_third = jnp.min(current, axis=3)]
    slice x15 -> x0, local copies, waits for them, and re-layouts: 18.4 us -> none  [the longest x8 11.8 us: advance(): padded = jnp.pad(center, ((0, 0), (0, 0), (0, 0), (2, 2)), mode='edge')]
    ppermute x4 -> x0, starting transfers between devices: 10.8 us -> none  [the longest x2 10.8 us: padded_2(): lax.ppermute(head, axis, [((i + 1) % count, i) for i in range(count)])]
    unnamed x24 -> x5, local copies, waits for them, and re-layouts: 16.2 us -> 6.49 us
    reshape x8 -> x0, local copies, waits for them, and re-layouts: 9.69 us -> none  [the longest x4 9.68 us: advance(): padded = jnp.pad(center, ((0, 0), (0, 0), (0, 0), (2, 2)), mode='edge')]
  transfers between devices with their start and end apart: 4 -> 0, of which waited for: 3 -> 0; matrix products, arithmetic and copies ran while one was open for 12% -> 0% of each run, Pallas kernels for 0% -> 0%
where the time goes in v1:
time: 170 us
  Pallas kernels  163 us (96%)
  local copies, waits for them, and re-layouts  6.49 us (4%)
    pallas_call x1, Pallas kernels, on_device(): pl.pallas_call(functools.partial(kernel, 'gx', 'sub'), out_shape=(jax.Sha...  163 us
    unnamed x5, local copies, waits for them, and re-layouts  6.49 us

profile of v1, /device:TPU:0, one launch (start us, length us, event | category | flops | bytes accessed | tf_op | source)
XLA Modules:
  0.0 169.9 jit_solution(2666385895279580400)
XLA Ops:
  0.6 1.3 copy.9.matrix
  1.9 162.8 %shard_map.86 = (f32[2,8,256,256]{3,2,1,0:T(8,128)}, f32[2,8,256]{2,1,0:T(8,128)}) custom-call(f32[2,8,256,256]{3,2,1,0:T(8,128)} %value.1, f32[2,8,256,256]{3,2,1,0:T(8,128)} %speed_in.1, f32[2,3,3]{2,1,0:T(4,128)} %copy.9.matrix, f32[2,3]{1,0:T(2,128)} %offset.1, f32[2,3]{1,0:T(2,128)} %bound.1, s32[8]{0:T(128)} %partner.1, s32[2]{0:T(128)} %dropped.1), custom_call_target="tpu_custom_call" | custom-call | tf_op jit(solution)/shard_map/pallas_call | solution.py:307
  164.7 0.0 copy-start
  164.7 4.6 %copy.12 = f32[2,8,256,256]{3,2,1,0:T(8,128)} copy(f32[2,8,256,256]{3,2,1,0:T(8,128)} %get-tuple-element.4) | data formatting | bytes 8388608
  169.3 0.0 copy-done
  169.3 0.6 copy.13
Async XLA Ops:
  164.7 4.6 %copy-start = (f32[2,8,256]{2,1,0:T(8,128)S(1)}, f32[2,8,256]{2,1,0:T(8,128)}, u32[]{:S(2)}) copy-start(f32[2,8,256]{2,1,0:T(8,128)} %get-tuple-element.5) | copy-start | bytes 49156

commit v2 on v1

--- a/solution.py
+++ b/solution.py
@@ -9,6 +9,7 @@
 
 STEPS = 2
 PAD = 8
+UNROLL = 4
 LANES = 128
 MESH = pl.DeviceIdType.MESH
 
@@ -29,29 +30,33 @@
     ]
 
 
-def lane_shift(parts, step, ends):
+def lane_lines(parts):
     lane = lax.broadcasted_iota(jnp.int32, parts[0].shape, 1)
-    rolled = [pltpu.roll(p, (LANES - step) % LANES, 1) for p in parts]
     count = len(parts)
-    if step == 1:
-        at_end = lane == LANES - 1
-        after = [rolled[i + 1] if i + 1 < count else ends for i in range(count)]
-    else:
-        at_end = lane == 0
-        after = [rolled[i - 1] if i > 0 else ends for i in range(count)]
-    return [jnp.where(at_end, after[i], rolled[i]) for i in range(count)]
-
-
-def lane_sides(parts):
-    zero = jnp.zeros_like(parts[0])
-    ahead = lane_shift(parts, 1, parts[-1])
-    slopes = [a - v for a, v in zip(ahead, parts)]
-    back_slopes = lane_shift(slopes, -1, zero)
-    curves = [a - b for a, b in zip(slopes, back_slopes)]
-    back_curves = lane_shift(curves, -1, zero)
-    picks = [pick(b, c, jnp.abs(b), jnp.abs(c)) for b, c in zip(back_curves, curves)]
-    ahead_picks = lane_shift(picks, 1, zero)
-    return [(b + q, a - s) for b, q, a, s in zip(back_slopes, picks, ahead_picks, slopes)]
+    rolled = {
+        step: [pltpu.roll(p, (LANES - step) % LANES, 1) for p in parts] for step in (-2, -1, 1, 2)
+    }
+    back_one = [
+        jnp.where(lane == 0, rolled[-1][i - 1] if i else parts[0], rolled[-1][i])
+        for i in range(count)
+    ]
+    back_two = [
+        jnp.where(lane < 2, rolled[-2][i - 1] if i else back_one[0], rolled[-2][i])
+        for i in range(count)
+    ]
+    ahead_one = [
+        jnp.where(
+            lane == LANES - 1, rolled[1][i + 1] if i + 1 < count else parts[i], rolled[1][i]
+        )
+        for i in range(count)
+    ]
+    ahead_two = [
+        jnp.where(
+            lane >= LANES - 2, rolled[2][i + 1] if i + 1 < count else ahead_one[i], rolled[2][i]
+        )
+        for i in range(count)
+    ]
+    return list(zip(back_two, back_one, parts, ahead_one, ahead_two))
 
 
 def kernel(
@@ -190,7 +195,7 @@
             new_lows = []
             for p in range(planes):
                 parts = [lines[h][p + 2] for h in range(halves)]
-                along_z = lane_sides(parts)
+                along_z = [sides(line)[0] for line in lane_lines(parts)]
                 new = []
                 for h in range(halves):
                     around = [
@@ -222,11 +227,11 @@
             return tuple(new_lows)
 
         if step == 0:
-            lax.fori_loop(0, cells_y // 8, block, ())
+            lax.fori_loop(0, cells_y // 8, block, (), unroll=UNROLL)
             pad_rows(second, s, start + 2, planes)
             return
         lows = tuple(jnp.full(tile, jnp.inf, jnp.float32) for _ in range(planes * halves))
-        lows = lax.fori_loop(0, cells_y // 8, block, lows)
+        lows = lax.fori_loop(0, cells_y // 8, block, lows, unroll=UNROLL)
         copy = pltpu.make_async_copy(
             result.at[s, pl.ds(start, planes)],
             final.at[s, pl.ds(start, planes)],

time: 170 us -> 126 us (0.74)
  Pallas kernels: 163 us -> 119 us
    pallas_call x1, Pallas kernels: 163 us -> 119 us  [on_device(): pl.pallas_call(functools.partial(kernel, 'gx', 'sub'), out_shape=(jax.Sha...]
where the time goes in v2:
time: 126 us
  Pallas kernels  119 us (94%)
  local copies, waits for them, and re-layouts  6.49 us (5%)
    pallas_call x1, Pallas kernels, on_device(): pl.pallas_call(functools.partial(kernel, 'gx', 'sub'), out_shape=(jax.Sha...  119 us
    unnamed x5, local copies, waits for them, and re-layouts  6.49 us

profile of v2, /device:TPU:0, one launch (start us, length us, event | category | flops | bytes accessed | tf_op | source)
XLA Modules:
  0.0 126.1 jit_solution(15922170779124249574)
XLA Ops:
  0.6 1.3 %copy.9.matrix = f32[2,3,3]{2,1,0:T(4,128)} copy(f32[2,3,3]{2,0,1:T(2,128)} %param.9) | data formatting | bytes 144 | tf_op args[2]
  1.9 119.0 %shard_map.86 = (f32[2,8,256,256]{3,2,1,0:T(8,128)}, f32[2,8,256]{2,1,0:T(8,128)}) custom-call(f32[2,8,256,256]{3,2,1,0:T(8,128)} %value.1, f32[2,8,256,256]{3,2,1,0:T(8,128)} %speed_in.1, f32[2,3,3]{2,1,0:T(4,128)} %copy.9.matrix, f32[2,3]{1,0:T(2,128)} %offset.1, f32[2,3]{1,0:T(2,128)} %bound.1, s32[8]{0:T(128)} %partner.1, s32[2]{0:T(128)} %dropped.1), custom_call_target="tpu_custom_call" | custom-call | tf_op jit(solution)/shard_map/pallas_call | solution.py:312
  120.9 0.0 copy-start
  120.9 4.6 %copy.12 = f32[2,8,256,256]{3,2,1,0:T(8,128)} copy(f32[2,8,256,256]{3,2,1,0:T(8,128)} %get-tuple-element.4) | data formatting | bytes 8388608
  125.5 0.0 copy-done
  125.5 0.6 copy.13
Async XLA Ops:
  120.9 4.6 %copy-start = (f32[2,8,256]{2,1,0:T(8,128)S(1)}, f32[2,8,256]{2,1,0:T(8,128)}, u32[]{:S(2)}) copy-start(f32[2,8,256]{2,1,0:T(8,128)} %get-tuple-element.5) | copy-start | bytes 49156

commit v3 on v2

--- a/solution.py
+++ b/solution.py
@@ -124,15 +124,15 @@
     sends = {}
 
     def send(step, s, side):
-        for h in range(halves):
-            start = rows - 2 if side == 0 else 0
-            land = 0 if side == 0 else rows + 2
+        start = rows - 2 if side == 0 else 0
+        land = 0 if side == 0 else rows + 2
+        for h in range(halves if step == 0 else 1):
             if step == 0:
                 source = value.at[s, pl.ds(start, 2), :, pl.ds(h * LANES, LANES)]
                 sink = first.at[s, pl.ds(land, 2), h, body, :]
             else:
-                source = second.at[s, pl.ds(start + 2, 2), h, body, :]
-                sink = second.at[s, pl.ds(land, 2), h, body, :]
+                source = second.at[s, pl.ds(start + 2, 2), :, body, :]
+                sink = second.at[s, pl.ds(land, 2), :, body, :]
             copy = pltpu.make_async_remote_copy(
                 src_ref=source,
                 dst_ref=sink,
@@ -145,7 +145,7 @@
             sends[step, s, side, h] = copy
 
     def receive(step, s, side):
-        for h in range(halves):
+        for h in range(halves if step == 0 else 1):
             sends[step, s, side, h].wait_recv()
 
     for s in range(subs):
@@ -263,20 +263,20 @@
     for s in range(subs):
         receive(0, s, 0)
         compute(0, s, 0, 2)
-        send(1, s, 1)
         receive(0, s, 1)
         compute(0, s, last, 2)
         send(1, s, 0)
+        send(1, s, 1)
     for s in range(subs):
         for start in range(2, last, 2):
             compute(1, s, start, 2)
 
     plane_sends = []
     for s in range(subs):
+        receive(1, s, 0)
+        compute(1, s, 0, 2)
         receive(1, s, 1)
         compute(1, s, last, 2)
-        receive(1, s, 0)
-        compute(1, s, 0, 2)
         gathered[sub_me * subs + s] = own[s]
         for k in range(1, sub_count):
             copy = pltpu.make_async_remote_copy(

time: 126 us -> 110 us (0.87)
  Pallas kernels: 119 us -> 102 us
    pallas_call x1, Pallas kernels: 119 us -> 102 us  [on_device(): pl.pallas_call(functools.partial(kernel, 'gx', 'sub'), out_shape=(jax.Sha...]
where the time goes in v3:
time: 110 us; the launch traced here: 109 us
  Pallas kernels  102 us (93%)
  local copies, waits for them, and re-layouts  6.49 us (6%)
    pallas_call x1, Pallas kernels, on_device(): pl.pallas_call(functools.partial(kernel, 'gx', 'sub'), out_shape=(jax.Sha...  102 us
    unnamed x5, local copies, waits for them, and re-layouts  6.49 us

profile of v3, /device:TPU:0, one launch (start us, length us, event | category | flops | bytes accessed | tf_op | source)
XLA Modules:
  0.0 109.1 jit_solution(9824929931783009463)
XLA Ops:
  0.6 1.3 %copy.9.matrix = f32[2,3,3]{2,1,0:T(4,128)} copy(f32[2,3,3]{2,0,1:T(2,128)} %param.9) | data formatting | bytes 144 | tf_op args[2]
  1.9 101.9 %shard_map.86 = (f32[2,8,256,256]{3,2,1,0:T(8,128)}, f32[2,8,256]{2,1,0:T(8,128)}) custom-call(f32[2,8,256,256]{3,2,1,0:T(8,128)} %value.1, f32[2,8,256,256]{3,2,1,0:T(8,128)} %speed_in.1, f32[2,3,3]{2,1,0:T(4,128)} %copy.9.matrix, f32[2,3]{1,0:T(2,128)} %offset.1, f32[2,3]{1,0:T(2,128)} %bound.1, s32[8]{0:T(128)} %partner.1, s32[2]{0:T(128)} %dropped.1), custom_call_target="tpu_custom_call" | custom-call | tf_op jit(solution)/shard_map/pallas_call | solution.py:312
  103.8 0.0 copy-start
  103.8 4.6 %copy.12 = f32[2,8,256,256]{3,2,1,0:T(8,128)} copy(f32[2,8,256,256]{3,2,1,0:T(8,128)} %get-tuple-element.4) | data formatting | bytes 8388608
  108.5 0.0 copy-done
  108.5 0.6 copy.13
Async XLA Ops:
  103.8 4.6 %copy-start = (f32[2,8,256]{2,1,0:T(8,128)S(1)}, f32[2,8,256]{2,1,0:T(8,128)}, u32[]{:S(2)}) copy-start(f32[2,8,256]{2,1,0:T(8,128)} %get-tuple-element.5) | copy-start | bytes 49156
